TPU v7x, 128 devices: a whole 4x4x4 slice. The times are simulated.
128 devices in a mesh: shard: 32 (over y, x, core), width: 4 (over z).
Axes of the slice: x: 4, y: 4, z: 4, core: 2. Of those that a mesh axis runs over, the one named last changes fastest.
Arguments:
- w_up: bfloat16 [12288, 49152], P('shard', 'width'), may hold values from -0.109375 to 0.109375
- low_up: bfloat16 [12288, 64], P('shard'), may hold values from -0.0546875 to 0.0546875
- high_up: bfloat16 [64, 49152], P(None, 'width'), may hold values from -0.75 to 0.75
- norm_train: float32 [12288], P(('shard', 'width')), may hold values from 0.25 to 1.75
- norm_step: float32 [12288], P(('shard', 'width')), may hold values from -0.3 to 0.3
Outputs:
- serve_up: bfloat16 [12288, 49152], P(None, ('width', 'shard'))
- scale_up: float32 [49152], P(('width', 'shard'))
- serve_norm: bfloat16 [12288], replicated
All inputs are finite; a program needn't handle non-finite values. Where the computation divides by a largest or mean magnitude, that divisor is 1e-20 or more.
Results may differ from a plain program's by a relative error of at most 0.001.
Values may be sent and summed in bfloat16 or wider, within the bound.
A program may use at most 128 MiB of HBM per device.

v0:
```python
import jax
import jax.numpy as jnp
from jax import lax
from jax.sharding import Mesh
from jax.sharding import PartitionSpec as P

D_MODEL = 12288
SHARD = ("shard_0", "shard_1", "shard_2")
SHARD_WIDTH = ("shard_0", "shard_1", "shard_2", "width")
WIDTH_SHARD = ("width", "shard_0", "shard_1", "shard_2")


mix_rate = 0.5


def from_everyone(array, axis):
    copies = jnp.broadcast_to(array, (lax.axis_size(axis), *array.shape))
    return lax.all_to_all(copies, axis, split_axis=0, concat_axis=0, tiled=True)


def of_everyone(array, axis):
    return from_everyone(array, axis).sum(axis=0)


def in_order(parts, dim):
    parts = jnp.moveaxis(parts, 0, dim)
    shape = parts.shape
    return parts.reshape(*shape[:dim], shape[dim] * shape[dim + 1], *shape[dim + 2 :])


def gather_in_order(array, axes, order):
    parts = array
    for k in order:
        parts = lax.all_gather(parts, axes[k])
    done = order[::-1]
    back = [done.index(k) for k in range(len(axes))]
    parts = parts.transpose(*back, *range(len(axes), parts.ndim))
    return parts.reshape(-1, *array.shape)


def gathered_by_axis(array, axes, order, dim):
    return in_order(gather_in_order(array, axes, order), dim)


def per_device(w_up, low_up, high_up, norm_train, norm_step):
    fresh_up = w_up.astype(jnp.float32) + mix_rate * jnp.dot(
        low_up, high_up, preferred_element_type=jnp.float32
    )
    total_up = of_everyone(jnp.sum(jnp.abs(fresh_up), axis=0), SHARD)
    scale_up = total_up / D_MODEL
    narrow_up = (fresh_up / scale_up).astype(jnp.bfloat16)
    serve_up = lax.all_to_all(narrow_up, SHARD, split_axis=1, concat_axis=0, tiled=True)
    place = lax.axis_index(SHARD)
    scale_up = lax.dynamic_slice_in_dim(scale_up, place * serve_up.shape[1], serve_up.shape[1])
    serve_norm = gathered_by_axis(
        (norm_train + norm_step).astype(jnp.bfloat16), SHARD_WIDTH, (0, 1, 3, 2), 0
    )
    return (serve_up, scale_up, serve_norm)


def solution(mesh):
    torus = Mesh(
        mesh.devices.reshape(4, 4, 2, mesh.shape["width"]),
        ("shard_0", "shard_1", "shard_2", "width"),
    )
    in_specs = (P(SHARD, "width"), P(SHARD, None), P(None, "width"), P(SHARD_WIDTH), P(SHARD_WIDTH))
    out_specs = (P(None, WIDTH_SHARD), P(WIDTH_SHARD), P())
    return jax.shard_map(
        per_device, mesh=torus, in_specs=in_specs, out_specs=out_specs, check_vma=False
    )
```

profile of v0, /device:TPU:0, one launch (start us, length us, event | category | flops | bytes accessed | tf_op | source)
XLA Modules:
  0.0 215.1 jit_solution(10589016466949314849)
XLA Ops:
  0.6 0.0 copy-start
  0.6 1.4 copy-done
  2.0 10.7 %abs_reduce_fusion = (f32[12288]{0:T(1024)S(1)}, f32[384,12288]{1,0:T(8,128)}) fusion(bf16[384,64]{0,1:T(8,128)(2,1)} %param.6, bf16[64,12288]{1,0:T(8,128)(2,1)S(1)} %copy-done, bf16[384,12288]{1,0:T(8,128)(2,1)} %param.5), kind=kOutput, calls=%fused_computation.1 | convolution fusion | flops 627560448 | bytes 29982720 | tf_op jit(solution)/shard_map/dot_general | solution.py:46
  12.7 1.4 broadcast_in_dim.4
  14.1 30.1 %all_to_all.25 = f32[32,1,12288]{2,1,0:T(1,128)S(1)} all-to-all(f32[32,1,12288]{2,1,0:T(1,128)S(1)} %broadcast_in_dim.4), channel_id=1, replica_groups=mesh['shard_0'=4,'shard_1'=4,'shard_2'=2,'width'=4] {'shard_0','shard_1'..., dimensions={0} | all-to-all | bytes 3145728 | tf_op jit(solution)/shard_map/all_to_all | solution.py:18
  44.2 1.0 reduce_sum.19
  45.3 11.5 %divide_convert_fusion = bf16[384,12288]{1,0:T(8,128)(2,1)} fusion(f32[384,12288]{1,0:T(8,128)} %get-tuple-element.4, f32[12288]{0:T(1024)S(1)} %broadcast_multiply_fusion), kind=kLoop, calls=%fused_computation | loop fusion | flops 9437184 | bytes 28360704 | tf_op jit(solution)/shard_map/convert_element_type | solution.py:51
  56.8 9.0 %copy.29 = bf16[48,32,8,384]{3,2,0,1:T(8,128)(2,1)} copy(bf16[48,32,8,384]{3,2,1,0:T(8,128)(2,1)} %bitcast.16) | data formatting | bytes 18874368 | tf_op jit(solution)/shard_map/all_to_all | solution.py:52
  65.8 0.0 copy-start.4
  65.8 0.0 copy-start.2
  65.8 0.0 copy-start.3
  65.8 5.1 %all-to-all-start.1 = ((bf16[384,32,384]{2,0,1:T(8,128)(2,1)}), bf16[384,32,384]{2,0,1:T(8,128)(2,1)}, u32[]{:S(2)}, u32[]{:S(2)}) async-start(bf16[384,32,384]{2,0,1:T(8,128)(2,1)} %bitcast.15), calls=%async_computation.1 | async-start | bytes 18874368 | tf_op jit(solution)/shard_map/all_to_all | solution.py:52
  70.9 0.0 copy-done.4
  70.9 0.6 dynamic-slice
  72.1 0.0 copy-done.2
  72.2 0.0 copy-done.3
  72.2 0.2 dynamic-update-slice
  72.4 109.8 %all-reduce = bf16[384]{0:T(512)(128)(2,1)S(1)} all-reduce(bf16[384]{0:T(512)(128)(2,1)S(1)} %dynamic-update-slice), channel_id=2, replica_groups=mesh['shard_0'=4,'shard_1'=4,'shard_2'=2,'width'=4] {'shard_0'}, use_global_device_ids=true, to_apply=%add | all-reduce | flops 384 | bytes 1536
  182.2 0.1 reshape.23
  182.3 7.0 %all-gather.4 = bf16[4,4,96]{2,1,0:T(4,128)(2,1)S(1)} all-gather(bf16[1,4,96]{2,1,0:T(4,128)(2,1)S(1)} %reshape.23), channel_id=3, replica_groups=mesh['shard_0'=4,'shard_1'=4,'shard_2'=2,'width'=4] {'shard_1'}, dimensions={0}, use_global_device_ids=true | all-gather | bytes 3840 | tf_op jit(solution)/shard_map/all_gather | solution.py:34
  189.3 13.2 %all-gather.2 = bf16[16,4,96]{2,1,0:T(4,128)(2,1)S(1)} all-gather(bf16[4,4,96]{2,1,0:T(4,128)(2,1)S(1)} %all-gather.4), channel_id=4, replica_groups=mesh['shard_0'=4,'shard_1'=4,'shard_2'=2,'width'=4] {'width'}, dimensions={0}, use_global_device_ids=true | all-gather | bytes 15360 | tf_op jit(solution)/shard_map/all_gather | solution.py:34
  202.5 1.8 all-gather.3
  204.3 0.7 reshape_reshape.3
  205.0 0.7 dynamic_slice.3
  205.7 0.0 all-to-all-done.1
  205.7 0.0 copy-start.1
  205.7 9.4 %copy.33 = bf16[12288,384]{1,0:T(8,128)(2,1)} copy(bf16[12288,384]{1,0:T(8,128)(2,1)} %bitcast.1) | data formatting | bytes 18874368
  215.1 0.0 copy-done.1
  (5 shorter events, 0.0 us)
Async XLA Ops:
  0.6 1.4 copy-start
  65.8 5.1 %copy-start.4 = (u32[128]{0:T(128)S(1)}, u32[128]{0:T(128)}, u32[]{:S(2)}) copy-start(u32[128]{0:T(128)} %constant.35) | copy-start | bytes 1540
  65.8 6.4 %copy-start.2 = (f32[96]{0:T(128)S(1)}, f32[96]{0:T(128)}, u32[]{:S(2)}) copy-start(f32[96]{0:T(128)} %param.8) | copy-start | bytes 1156
  65.8 6.4 %copy-start.3 = (f32[96]{0:T(128)S(1)}, f32[96]{0:T(128)}, u32[]{:S(2)}) copy-start(f32[96]{0:T(128)} %param.9) | copy-start | bytes 1156
  65.8 139.9 %all-to-all-start.1 = ((bf16[384,32,384]{2,0,1:T(8,128)(2,1)}), bf16[384,32,384]{2,0,1:T(8,128)(2,1)}, u32[]{:S(2)}, u32[]{:S(2)}) async-start(bf16[384,32,384]{2,0,1:T(8,128)(2,1)} %bitcast.15), calls=%async_computation.1 | async-start | bytes 18874368 | tf_op jit(solution)/shard_map/all_to_all | solution.py:52
  205.7 9.4 %copy-start.1 = (bf16[64,12288]{1,0:T(8,128)(2,1)S(1)}, bf16[64,12288]{1,0:T(8,128)(2,1)}, u32[]{:S(2)}) copy-start(bf16[64,12288]{1,0:T(8,128)(2,1)} %param.7) | copy-start | bytes 4718596
where the time goes:
time: 217 us; the launch traced here: 215 us
  blocking collectives  162 us (75%)
  local copies, waits for them, and re-layouts  23.5 us (11%)
  other arithmetic  12.6 us (6%)
  matrix products  10.7 us (5%)
  starting transfers between devices  5.11 us (2%)
    unnamed x1, blocking collectives  110 us
    all_to_all x1, blocking collectives, from_everyone(): return lax.all_to_all(copies, axis, split_axis=0, concat_axis=0, tiled=True)  30.1 us
    all_gather x3, blocking collectives, gather_in_order(): parts = lax.all_gather(parts, axes[k])  22 us
    unnamed x15, local copies, waits for them, and re-layouts  11.7 us
    convert_element_type x1, other arithmetic, per_device(): narrow_up = (fresh_up / scale_up).astype(jnp.bfloat16)  11.5 us
    dot_general x1, matrix products, per_device(): jnp.dot(low_up, high_up, preferred_element_type=jnp.float32)  10.7 us
    all_to_all x1, local copies, waits for them, and re-layouts, per_device(): lax.all_to_all(narrow_up, SHARD, split_axis=1, concat_axis=0, tiled=True)  8.99 us
    all_to_all x1, starting transfers between devices, per_device(): lax.all_to_all(narrow_up, SHARD, split_axis=1, concat_axis=0, tiled=True)  5.11 us
  transfers between devices with their start and end apart: 1, of which 0 were waited for; matrix products, arithmetic and copies ran while one was open for 1% of the time, Pallas kernels for 0%

commit v1 on v0

v1 whole, which is shorter than its diff:
```python
import functools

import jax
import jax.numpy as jnp
from jax import lax
from jax.experimental import pallas as pl
from jax.experimental.pallas import tpu as pltpu
from jax.sharding import Mesh
from jax.sharding import PartitionSpec as P

D_MODEL = 12288
RANK = 64
SIDE = 4
CORES = 2
CHIPS = SIDE * SIDE
GROUP = CHIPS * CORES
ROWS = D_MODEL // GROUP
COLS = 384
PIECE = RANK // SIDE
NORM = 96
STEP = 128
SHARD = ("shard_0", "shard_1", "shard_2")
SHARD_WIDTH = ("shard_0", "shard_1", "shard_2", "width")
WIDTH_SHARD = ("width", "shard_0", "shard_1", "shard_2")
MESH = pl.DeviceIdType.MESH

mix_rate = 0.5


def hops(*pairs):
    def wrapped(v):
        return tuple(q % SIDE for q in v) if isinstance(v, tuple) else (v % SIDE,) * 2

    return [(wrapped(dy), wrapped(dx), dc) for dc in range(CORES) for dy, dx in pairs]


STAGES = [
    hops((1, 1), (-1, -1)) + [((0, 0), (0, 0), 1)],
    hops((1, -1), (-1, 1)),
    hops((0, 2), (2, 0)),
    hops((2, 2)),
    hops((1, 2), (-1, 2), (1, 0), (-1, 0)),
    hops(((2, 0), 1), ((2, 0), -1)),
    hops(((0, 2), 1), ((0, 2), -1)),
]
FIRST = [sum(len(s) for s in STAGES[:k]) for k in range(len(STAGES) + 1)]
AHEAD = 2


def by_core(core, value):
    return value[0] if value[0] == value[1] else jnp.where(core == 0, value[0], value[1])


def exchange(
    w, low, high, train, step,
    rows, lows, own_high, scale, norms,
    norm_own, norm_z, norm_mid, total,
    send, recv, low_send, low_recv, low_zsend, low_zrecv, nz_send, nz_recv, n_send, n_recv, local,
):
    y, x, core = (lax.axis_index(a) for a in SHARD)
    z = lax.axis_index("width")
    chip = y * SIDE + x
    me = chip * CORES + core

    def at(dy, dx, dc):
        return lax.rem(y + dy, SIDE), lax.rem(x + dx, SIDE), lax.rem(core + dc, CORES)

    def device(ty, tx, tc, tz=None):
        return {"shard_0": ty, "shard_1": tx, "shard_2": tc, "width": z if tz is None else tz}

    plane = [(dy, dx, dc) for dy in range(SIDE) for dx in range(SIDE) for dc in range(CORES)][1:]
    column = [(dz, dc) for dz in range(SIDE) for dc in range(CORES)][1:]

    get_high = pltpu.make_async_copy(
        high.at[:, pl.ds(pl.multiple_of(me * COLS, 128), COLS)], own_high, local.at[0]
    )
    get_high.start()
    get_rows = pltpu.make_async_copy(
        w.at[:, pl.ds(pl.multiple_of(me * COLS, 128), COLS)],
        rows.at[pl.ds(pl.multiple_of(me * ROWS, ROWS), ROWS), :],
        local.at[1],
    )
    get_rows.start()
    get_low = pltpu.make_async_copy(
        low.at[pl.ds(pl.multiple_of(z * PIECE, PIECE), PIECE), :], lows.at[z, core, chip], local.at[2]
    )
    get_low.start()
    norm_own[...] = jnp.zeros_like(norm_own)
    norm_own[0, :, 0:NORM] = (train[...] + step[...]).astype(jnp.bfloat16).astype(jnp.float32)

    barrier = pltpu.get_barrier_semaphore()
    for dy, dx, dc in plane:
        pl.semaphore_signal(barrier, inc=1, device_id=device(*at(dy, dx, dc)), device_id_type=MESH)
    for dz, dc in column[1:]:
        to = device(y, x, lax.rem(core + dc, CORES), lax.rem(z + dz, SIDE))
        pl.semaphore_signal(barrier, inc=1, device_id=to, device_id_type=MESH)
    pl.semaphore_wait(barrier, len(plane) + len(column) - 1)

    low_copies = []
    for k, (dy, dx, dc) in enumerate([h for h in plane if h[2] == 0]):
        low_copies.append(
            pltpu.make_async_remote_copy(
                src_ref=low.at[pl.ds(pl.multiple_of(z * PIECE, PIECE), PIECE), :],
                dst_ref=lows.at[z, core, chip],
                send_sem=low_send.at[k],
                recv_sem=low_recv.at[k],
                device_id=device(*at(dy, dx, 0)),
                device_id_type=MESH,
            )
        )
    for c in low_copies:
        c.start()
    nz_copies = [
        pltpu.make_async_remote_copy(
            src_ref=norm_own.at[0],
            dst_ref=norm_z.at[z],
            send_sem=nz_send.at[dz - 1],
            recv_sem=nz_recv.at[dz - 1],
            device_id=device(y, x, core, lax.rem(z + dz, SIDE)),
            device_id_type=MESH,
        )
        for dz in range(1, SIDE)
    ]
    for c in nz_copies:
        c.start()
    norm_z[z] = norm_own[0]

    def row_copy(i, hop):
        ty, tx, tc = at(by_core(core, hop[0]), by_core(core, hop[1]), hop[2])
        to = (ty * SIDE + tx) * CORES + tc
        return pltpu.make_async_remote_copy(
            src_ref=w.at[:, pl.ds(pl.multiple_of(to * COLS, 128), COLS)],
            dst_ref=rows.at[pl.ds(pl.multiple_of(me * ROWS, ROWS), ROWS), :],
            send_sem=send.at[i],
            recv_sem=recv.at[i],
            device_id=device(ty, tx, tc),
            device_id_type=MESH,
        )

    copies = [[row_copy(FIRST[k] + i, hop) for i, hop in enumerate(s)] for k, s in enumerate(STAGES)]

    def start(k):
        if k >= AHEAD:
            for c in copies[k - AHEAD]:
                c.wait_send()
        for c in copies[k]:
            c.start()

    def add_block(source_chip, source_core):
        base = (source_chip * CORES + source_core) * ROWS
        for r in range(0, ROWS, STEP):
            left = lows[:, source_core, source_chip, :, r : r + STEP].reshape(RANK, STEP)
            change = lax.dot_general(
                left, own_high[...], (((0,), (0,)), ((), ())), preferred_element_type=jnp.float32
            )
            fresh = rows[pl.ds(pl.multiple_of(base + r, STEP), STEP), :].astype(jnp.float32) + change
            total[...] += jnp.abs(fresh).reshape(STEP // 8, 8, COLS).sum(axis=0)

    def take(k):
        stage = STAGES[k]

        def one(i, carry):
            def pick(values):
                out = values[0]
                for j in range(1, len(values)):
                    out = jnp.where(i == j, values[j], out)
                return out

            dc = pick([h[2] for h in stage])
            source_core = lax.rem(core + dc, CORES)
            dy = jnp.where(source_core == 0, pick([h[0][0] for h in stage]), pick([h[0][1] for h in stage]))
            dx = jnp.where(source_core == 0, pick([h[1][0] for h in stage]), pick([h[1][1] for h in stage]))
            source_chip = lax.rem(y + SIDE - dy, SIDE) * SIDE + lax.rem(x + SIDE - dx, SIDE)
            base = (source_chip * CORES + source_core) * ROWS
            landed = rows.at[pl.ds(pl.multiple_of(base, ROWS), ROWS), :]
            pltpu.make_async_copy(landed, landed, recv.at[FIRST[k] + i]).wait()
            add_block(source_chip, source_core)
            return carry

        lax.fori_loop(0, len(stage), one, 0)

    start(0)
    start(1)

    get_low.wait()
    for c in low_copies:
        c.wait_recv()
    low_zcopies = []
    for k, (dz, dc) in enumerate(column):
        low_zcopies.append(
            pltpu.make_async_remote_copy(
                src_ref=lows.at[z, core],
                dst_ref=lows.at[z, core],
                send_sem=low_zsend.at[k],
                recv_sem=low_zrecv.at[k],
                device_id=device(y, x, lax.rem(core + dc, CORES), lax.rem(z + dz, SIDE)),
                device_id_type=MESH,
            )
        )
    for c in low_zcopies:
        c.start()

    for c in nz_copies:
        c.wait_recv()
    lane = lax.broadcasted_iota(jnp.int32, (1, 128), 1)
    second = pltpu.roll(norm_z[1], NORM, 1)
    third = pltpu.roll(norm_z[2], 64, 1)
    fourth = pltpu.roll(norm_z[3], 32, 1)
    norm_mid[0] = jnp.where(lane < NORM, norm_z[0], second)
    norm_mid[1] = jnp.where(lane < 64, second, third)
    norm_mid[2] = jnp.where(lane < 32, third, fourth)
    for j in range(3):
        norms[me * 3 + j] = norm_mid[j]
    own_high[...] = own_high_half(get_high, own_high)
    total[...] = jnp.zeros_like(total)

    start(2)
    norm_copies = [
        pltpu.make_async_remote_copy(
            src_ref=norm_mid,
            dst_ref=norms.at[pl.ds(me * 3, 3)],
            send_sem=n_send.at[k],
            recv_sem=n_recv.at[k],
            device_id=device(*at(dy, dx, dc)),
            device_id_type=MESH,
        )
        for k, (dy, dx, dc) in enumerate(plane)
    ]
    for c in norm_copies:
        c.start()
    start(3)
    for c in low_zcopies:
        c.wait_recv()
    get_rows.wait()
    add_block(chip, core)
    take(0)
    start(4)
    take(1)
    start(5)
    take(2)
    start(6)
    for k in range(3, len(STAGES)):
        take(k)
    for k in range(len(STAGES) - AHEAD, len(STAGES)):
        for c in copies[k]:
            c.wait_send()
    for c in low_copies + low_zcopies + nz_copies + norm_copies:
        c.wait_send()
    for c in norm_copies:
        c.wait_recv()
    scale[...] = total[...].sum(axis=0, keepdims=True) / D_MODEL


def own_high_half(copy, own_high):
    copy.wait()
    return (own_high[...].astype(jnp.float32) * mix_rate).astype(jnp.bfloat16)


SLOTS = 4


def finish(rows, lows, own_high, scale, norms, serve, scale_out, norm_out, slots, sems):
    scale_out[...] = scale[...]
    norm_out[...] = norms[...].reshape(D_MODEL // 128, 128).astype(jnp.bfloat16)
    inverse = 1.0 / scale[...]

    def put(n, slot):
        to = serve.at[pl.ds(pl.multiple_of(n * ROWS, ROWS), ROWS), :]
        return pltpu.make_async_copy(slots.at[slot], to, sems.at[slot])

    def one(n, carry):
        slot = lax.rem(n, SLOTS)

        @pl.when(n >= SLOTS)
        def _():
            put(n - SLOTS, slot).wait()

        source_chip, source_core = n // CORES, lax.rem(n, CORES)
        for r in range(0, ROWS, STEP):
            left = lows[:, source_core, source_chip, :, r : r + STEP].reshape(RANK, STEP)
            change = lax.dot_general(
                left, own_high[...], (((0,), (0,)), ((), ())), preferred_element_type=jnp.float32
            )
            fresh = rows[pl.ds(pl.multiple_of(n * ROWS + r, STEP), STEP), :].astype(jnp.float32) + change
            slots[slot, r : r + STEP, :] = (fresh * inverse).astype(jnp.bfloat16)
        put(n, slot).start()
        return carry

    lax.fori_loop(0, GROUP, one, 0)
    for n in range(GROUP - SLOTS, GROUP):
        put(n, n % SLOTS).wait()


def per_device(w_up, low_up, high_up, norm_train, norm_step):
    dma = pltpu.SemaphoreType.DMA
    anywhere = pl.BlockSpec(memory_space=pl.ANY)
    vmem = pl.BlockSpec(memory_space=pltpu.VMEM)
    chips = CHIPS - 1
    column = SIDE * CORES - 1
    total = FIRST[-1]
    gathered = pl.pallas_call(
        exchange,
        out_shape=(
            pltpu.VMEM((D_MODEL, COLS), jnp.bfloat16),
            pltpu.VMEM((SIDE, CORES, CHIPS, PIECE, ROWS), jnp.bfloat16),
            pltpu.VMEM((RANK, COLS), jnp.bfloat16),
            pltpu.VMEM((1, COLS), jnp.float32),
            pltpu.VMEM((D_MODEL // 128, 1, 128), jnp.float32),
        ),
        in_specs=[anywhere, anywhere, anywhere, vmem, vmem],
        out_specs=(vmem,) * 5,
        scratch_shapes=[
            pltpu.VMEM((1, 1, 128), jnp.float32),
            pltpu.VMEM((SIDE, 1, 128), jnp.float32),
            pltpu.VMEM((3, 1, 128), jnp.float32),
            pltpu.VMEM((8, COLS), jnp.float32),
            dma((total,)),
            dma((total,)),
            dma((chips,)),
            dma((chips,)),
            dma((column,)),
            dma((column,)),
            dma((SIDE - 1,)),
            dma((SIDE - 1,)),
            dma((GROUP - 1,)),
            dma((GROUP - 1,)),
            dma((3,)),
        ],
        compiler_params=pltpu.CompilerParams(
            collective_id=0, has_side_effects=True, vmem_limit_bytes=8 * 2**20
        ),
        name="exchange",
    )(w_up, low_up.T, high_up, norm_train.reshape(1, NORM), norm_step.reshape(1, NORM))
    serve_up, scale_up, serve_norm = pl.pallas_call(
        finish,
        out_shape=(
            jax.ShapeDtypeStruct((D_MODEL, COLS), jnp.bfloat16),
            jax.ShapeDtypeStruct((1, COLS), jnp.float32),
            jax.ShapeDtypeStruct((D_MODEL // 128, 128), jnp.bfloat16),
        ),
        in_specs=[vmem] * 5,
        out_specs=(anywhere, vmem, vmem),
        scratch_shapes=[pltpu.VMEM((SLOTS, ROWS, COLS), jnp.bfloat16), dma((SLOTS,))],
        compiler_params=pltpu.CompilerParams(vmem_limit_bytes=16 * 2**20),
        name="finish",
    )(*gathered)
    return serve_up, scale_up.reshape(COLS), serve_norm.reshape(D_MODEL)


def solution(mesh):
    torus = Mesh(
        mesh.devices.reshape(SIDE, SIDE, CORES, mesh.shape["width"]),
        ("shard_0", "shard_1", "shard_2", "width"),
    )
    in_specs = (P(SHARD, "width"), P(SHARD, None), P(None, "width"), P(SHARD_WIDTH), P(SHARD_WIDTH))
    out_specs = (P(None, WIDTH_SHARD), P(WIDTH_SHARD), P())
    return jax.shard_map(
        per_device, mesh=torus, in_specs=in_specs, out_specs=out_specs, check_vma=False
    )
```

time: 217 us -> 137 us (0.63)
  blocking collectives: 162 us -> 0 us
  Pallas kernels: 0 us -> 128 us
  local copies, waits for them, and re-layouts: 23.5 us -> 7.19 us
  other arithmetic: 12.6 us -> 0.6 us
  matrix products: 10.7 us -> 0 us
  starting transfers between devices: 5.11 us -> 0 us
    pallas_call x0 -> x2, Pallas kernels: none -> 128 us  [the longest x1 118 us: per_device(): pl.pallas_call(exchange, out_shape=(pltpu.VMEM((D_MODEL, COLS), jnp.bfloa...]
    unnamed x1 -> x0, blocking collectives: 110 us -> none
    all_to_all x1 -> x0, blocking collectives: 30.1 us -> none  [from_everyone(): return lax.all_to_all(copies, axis, split_axis=0, concat_axis=0, tiled=True)]
    all_gather x3 -> x0, blocking collectives: 22 us -> none  [gather_in_order(): parts = lax.all_gather(parts, axes[k])]
    convert_element_type x2 -> x0, other arithmetic: 11.5 us -> none  [the longest x1 11.5 us: per_device(): narrow_up = (fresh_up / scale_up).astype(jnp.bfloat16)]
    dot_general x1 -> x0, matrix products: 10.7 us -> none  [per_device(): jnp.dot(low_up, high_up, preferred_element_type=jnp.float32)]
    all_to_all x1 -> x0, local copies, waits for them, and re-layouts: 8.99 us -> none  [per_device(): lax.all_to_all(narrow_up, SHARD, split_axis=1, concat_axis=0, tiled=True)]
    all_to_all x1 -> x0, starting transfers between devices: 5.11 us -> none  [per_device(): lax.all_to_all(narrow_up, SHARD, split_axis=1, concat_axis=0, tiled=True)]
  transfers between devices with their start and end apart: 1 -> 0, of which waited for: 0 -> 0; matrix products, arithmetic and copies ran while one was open for 1% -> 0% of each run, Pallas kernels for 0% -> 0%
where the time goes in v1:
time: 137 us; the launch traced here: 136 us
  Pallas kernels  128 us (93%)
  local copies, waits for them, and re-layouts  7.19 us (5%)
    pallas_call x1, Pallas kernels, per_device(): pl.pallas_call(exchange, out_shape=(pltpu.VMEM((D_MODEL, COLS), jnp.bfloa...  118 us
    pallas_call x1, Pallas kernels, per_device(): pl.pallas_call(finish, out_shape=(jax.ShapeDtypeStruct((D_MODEL, COLS), j...  10.4 us
    unnamed x10, local copies, waits for them, and re-layouts  7.19 us

profile of v1, /device:TPU:0, one launch (start us, length us, event | category | flops | bytes accessed | tf_op | source)
XLA Modules:
  0.0 136.5 jit_solution(13134079287628770146)
XLA Ops:
  0.6 0.0 copy-start
  0.6 3.7 %copy-done = bf16[384,12288]{1,0:T(8,128)(2,1)S(1)} copy-done((bf16[384,12288]{1,0:T(8,128)(2,1)S(1)}, bf16[384,12288]{1,0:T(8,128)(2,1)}, u32[]{:S(2)}) %copy-start) | copy-done | bytes 9437208
  4.3 0.0 copy-start.1
  4.3 1.4 %copy-done.1 = bf16[64,12288]{1,0:T(8,128)(2,1)S(1)} copy-done((bf16[64,12288]{1,0:T(8,128)(2,1)S(1)}, bf16[64,12288]{1,0:T(8,128)(2,1)}, u32[]{:S(2)}) %copy-start.1) | copy-done | bytes 1572888
  5.7 0.0 copy-start.2
  5.7 0.8 copy-done.2
  6.5 0.0 copy-start.3
  6.5 0.7 copy-done.3
  7.2 0.0 copy-start.4
  7.2 0.7 copy-done.4
  7.8 117.6 %exchange.1 = (bf16[12288,384]{1,0:T(8,128)(2,1)S(1)}, bf16[4,2,16,16,384]{4,3,2,1,0:T(8,128)(2,1)S(1)}, bf16[64,384]{1,0:T(8,128)(2,1)S(1)}, f32[1,384]{1,0:T(1,128)S(1)}, f32[96,1,128]{2,1,0:T(1,128)S(1)}) custom-call(bf16[384,12288]{1,0:T(8,128)(2,1)S(1)} %copy-done, bf16[64,384]{1,0:T(8,128)(2,1)S(1)} %bitcast.4, bf16[64,12288]{1,0:T(8,128)(2,1)S(1)} %copy-done.1, ...), custom_call_target="tpu_custom_call" | custom-call | tf_op jit(solution)/shard_map/exchange/pallas_call | solution.py:301
  125.4 10.4 %finish.1 = (bf16[12288,384]{1,0:T(8,128)(2,1)}, f32[1,384]{1,0:T(1,128)S(1)}, bf16[96,128]{1,0:T(8,128)(2,1)}) custom-call(bf16[12288,384]{1,0:T(8,128)(2,1)S(1)} %get-tuple-element.11.rows, bf16[4,2,16,16,384]{4,3,2,1,0:T(8,128)(2,1)S(1)} %get-tuple-element.12.lows, bf16[64,384]{1,0:T(8,128)(2,1)S(1)} %get-tuple-element.13.own_high, ...), custom_call_target="tpu_custom_call" | custom-call | tf_op jit(solution)/shard_map/finish/pallas_call | solution.py:334
  135.9 0.6 reduce
Async XLA Ops:
  0.6 3.7 %copy-start = (bf16[384,12288]{1,0:T(8,128)(2,1)S(1)}, bf16[384,12288]{1,0:T(8,128)(2,1)}, u32[]{:S(2)}) copy-start(bf16[384,12288]{1,0:T(8,128)(2,1)} %w.1) | copy-start | bytes 28311556
  4.3 1.4 %copy-start.1 = (bf16[64,12288]{1,0:T(8,128)(2,1)S(1)}, bf16[64,12288]{1,0:T(8,128)(2,1)}, u32[]{:S(2)}) copy-start(bf16[64,12288]{1,0:T(8,128)(2,1)} %high.1) | copy-start | bytes 4718596
  5.7 0.8 copy-start.2
  6.5 0.7 copy-start.3
  7.2 0.7 copy-start.4

commit v2 on v1

--- a/solution.py
+++ b/solution.py
@@ -53,8 +53,8 @@
 
 def exchange(
     w, low, high, train, step,
-    rows, lows, own_high, scale, norms,
-    norm_own, norm_z, norm_mid, total,
+    fresh_out, scale, norms,
+    rows, lows, own_high, norm_in, norm_own, norm_z, norm_mid, total,
     send, recv, low_send, low_recv, low_zsend, low_zrecv, nz_send, nz_recv, n_send, n_recv, local,
 ):
     y, x, core = (lax.axis_index(a) for a in SHARD)
@@ -85,8 +85,12 @@
         low.at[pl.ds(pl.multiple_of(z * PIECE, PIECE), PIECE), :], lows.at[z, core, chip], local.at[2]
     )
     get_low.start()
+    get_norms = [
+        pltpu.make_async_copy(part, norm_in.at[k], local.at[3 + k]) for k, part in enumerate((train, step))
+    ]
+    for c in get_norms:
+        c.start()
     norm_own[...] = jnp.zeros_like(norm_own)
-    norm_own[0, :, 0:NORM] = (train[...] + step[...]).astype(jnp.bfloat16).astype(jnp.float32)
 
     barrier = pltpu.get_barrier_semaphore()
     for dy, dx, dc in plane:
@@ -110,6 +114,9 @@
         )
     for c in low_copies:
         c.start()
+    for c in get_norms:
+        c.wait()
+    norm_own[0, :, 0:NORM] = (norm_in[0] + norm_in[1]).astype(jnp.bfloat16).astype(jnp.float32)
     nz_copies = [
         pltpu.make_async_remote_copy(
             src_ref=norm_own.at[0],
@@ -121,9 +128,6 @@
         )
         for dz in range(1, SIDE)
     ]
-    for c in nz_copies:
-        c.start()
-    norm_z[z] = norm_own[0]
 
     def row_copy(i, hop):
         ty, tx, tc = at(by_core(core, hop[0]), by_core(core, hop[1]), hop[2])
@@ -154,6 +158,7 @@
                 left, own_high[...], (((0,), (0,)), ((), ())), preferred_element_type=jnp.float32
             )
             fresh = rows[pl.ds(pl.multiple_of(base + r, STEP), STEP), :].astype(jnp.float32) + change
+            fresh_out[pl.ds(pl.multiple_of(base + r, STEP), STEP), :] = fresh
             total[...] += jnp.abs(fresh).reshape(STEP // 8, 8, COLS).sum(axis=0)
 
     def take(k):
@@ -182,6 +187,9 @@
     start(0)
     start(1)
 
+    for c in nz_copies:
+        c.start()
+    norm_z[z] = norm_own[0]
     get_low.wait()
     for c in low_copies:
         c.wait_recv()
@@ -259,10 +267,10 @@
 SLOTS = 4
 
 
-def finish(rows, lows, own_high, scale, norms, serve, scale_out, norm_out, slots, sems):
-    scale_out[...] = scale[...]
+def finish(fresh, scale, norms, serve, scale_out, norm_out, slots, sems):
+    scale_out[...] = scale[...].reshape(COLS)
     norm_out[...] = norms[...].reshape(D_MODEL // 128, 128).astype(jnp.bfloat16)
-    inverse = 1.0 / scale[...]
+    inverse = jnp.broadcast_to(1.0 / scale[...], (8, COLS))
 
     def put(n, slot):
         to = serve.at[pl.ds(pl.multiple_of(n * ROWS, ROWS), ROWS), :]
@@ -275,14 +283,8 @@
         def _():
             put(n - SLOTS, slot).wait()
 
-        source_chip, source_core = n // CORES, lax.rem(n, CORES)
-        for r in range(0, ROWS, STEP):
-            left = lows[:, source_core, source_chip, :, r : r + STEP].reshape(RANK, STEP)
-            change = lax.dot_general(
-                left, own_high[...], (((0,), (0,)), ((), ())), preferred_element_type=jnp.float32
-            )
-            fresh = rows[pl.ds(pl.multiple_of(n * ROWS + r, STEP), STEP), :].astype(jnp.float32) + change
-            slots[slot, r : r + STEP, :] = (fresh * inverse).astype(jnp.bfloat16)
+        part = fresh[pl.ds(pl.multiple_of(n * ROWS, ROWS), ROWS), :].reshape(ROWS // 8, 8, COLS)
+        slots[slot] = (part * inverse).reshape(ROWS, COLS).astype(jnp.bfloat16)
         put(n, slot).start()
         return carry
 
@@ -293,23 +295,25 @@
 
 def per_device(w_up, low_up, high_up, norm_train, norm_step):
     dma = pltpu.SemaphoreType.DMA
-    anywhere = pl.BlockSpec(memory_space=pl.ANY)
     vmem = pl.BlockSpec(memory_space=pltpu.VMEM)
     chips = CHIPS - 1
     column = SIDE * CORES - 1
     total = FIRST[-1]
+    operands = (w_up, low_up.T, high_up, norm_train.reshape(1, NORM), norm_step.reshape(1, NORM))
     gathered = pl.pallas_call(
         exchange,
         out_shape=(
+            pltpu.VMEM((D_MODEL, COLS), jnp.float32),
+            pltpu.VMEM((1, COLS), jnp.float32),
+            pltpu.VMEM((D_MODEL // 128, 1, 128), jnp.float32),
+        ),
+        in_specs=[pl.BlockSpec(memory_space=pltpu.HBM)] * 5,
+        out_specs=(vmem,) * 3,
+        scratch_shapes=[
             pltpu.VMEM((D_MODEL, COLS), jnp.bfloat16),
             pltpu.VMEM((SIDE, CORES, CHIPS, PIECE, ROWS), jnp.bfloat16),
             pltpu.VMEM((RANK, COLS), jnp.bfloat16),
-            pltpu.VMEM((1, COLS), jnp.float32),
-            pltpu.VMEM((D_MODEL // 128, 1, 128), jnp.float32),
-        ),
-        in_specs=[anywhere, anywhere, anywhere, vmem, vmem],
-        out_specs=(vmem,) * 5,
-        scratch_shapes=[
+            pltpu.VMEM((2, 1, NORM), jnp.float32),
             pltpu.VMEM((1, 1, 128), jnp.float32),
             pltpu.VMEM((SIDE, 1, 128), jnp.float32),
             pltpu.VMEM((3, 1, 128), jnp.float32),
@@ -324,27 +328,27 @@
             dma((SIDE - 1,)),
             dma((GROUP - 1,)),
             dma((GROUP - 1,)),
-            dma((3,)),
+            dma((5,)),
         ],
         compiler_params=pltpu.CompilerParams(
-            collective_id=0, has_side_effects=True, vmem_limit_bytes=8 * 2**20
+            collective_id=0, has_side_effects=True, vmem_limit_bytes=20 * 2**20
         ),
         name="exchange",
-    )(w_up, low_up.T, high_up, norm_train.reshape(1, NORM), norm_step.reshape(1, NORM))
+    )(*(pltpu.with_memory_space_constraint(a, pltpu.HBM) for a in operands))
     serve_up, scale_up, serve_norm = pl.pallas_call(
         finish,
         out_shape=(
             jax.ShapeDtypeStruct((D_MODEL, COLS), jnp.bfloat16),
-            jax.ShapeDtypeStruct((1, COLS), jnp.float32),
+            jax.ShapeDtypeStruct((COLS,), jnp.float32),
             jax.ShapeDtypeStruct((D_MODEL // 128, 128), jnp.bfloat16),
         ),
-        in_specs=[vmem] * 5,
-        out_specs=(anywhere, vmem, vmem),
+        in_specs=[vmem] * 3,
+        out_specs=(pl.BlockSpec(memory_space=pltpu.HBM), vmem, vmem),
         scratch_shapes=[pltpu.VMEM((SLOTS, ROWS, COLS), jnp.bfloat16), dma((SLOTS,))],
-        compiler_params=pltpu.CompilerParams(vmem_limit_bytes=16 * 2**20),
+        compiler_params=pltpu.CompilerParams(vmem_limit_bytes=6 * 2**20),
         name="finish",
     )(*gathered)
-    return serve_up, scale_up.reshape(COLS), serve_norm.reshape(D_MODEL)
+    return serve_up, scale_up, serve_norm.reshape(D_MODEL)
 
 
 def solution(mesh):

time: 137 us -> 126 us (0.920)
  local copies, waits for them, and re-layouts: 7.19 us -> 0 us
  Pallas kernels: 128 us -> 125 us
    unnamed x10 -> x0, local copies, waits for them, and re-layouts: 7.19 us -> none
    pallas_call x1, Pallas kernels: 10.4 us -> 7 us  [per_device(): pl.pallas_call(finish, out_shape=(jax.ShapeDtypeStruct((D_MODEL, COLS), j...]
where the time goes in v2:
time: 126 us; the launch traced here: 125 us
  Pallas kernels  125 us (99%)
    pallas_call x1, Pallas kernels, per_device(): pl.pallas_call(exchange, out_shape=(pltpu.VMEM((D_MODEL, COLS), jnp.float...  118 us
    pallas_call x1, Pallas kernels, per_device(): pl.pallas_call(finish, out_shape=(jax.ShapeDtypeStruct((D_MODEL, COLS), j...  7 us

profile of v2, /device:TPU:0, one launch (start us, length us, event | category | flops | bytes accessed | tf_op | source)
XLA Modules:
  0.0 125.5 jit_solution(3084865077370617003)
XLA Ops:
  0.6 117.9 %exchange.1 = (f32[12288,384]{1,0:T(8,128)S(1)}, f32[1,384]{1,0:T(1,128)S(1)}, f32[96,1,128]{2,1,0:T(1,128)S(1)}) custom-call(bf16[384,12288]{1,0:T(8,128)(2,1)} %w.1, bf16[64,384]{1,0:T(8,128)(2,1)} %bitcast.4, bf16[64,12288]{1,0:T(8,128)(2,1)} %high.1, f32[1,96]{1,0:T(1,128)} %bitcast.5, f32[1,96]{1,0:T(1,128)} %bitcast.6), custom_call_target="tpu_custom_call" | custom-call | tf_op jit(solution)/shard_map/exchange/pallas_call | solution.py:303
  118.5 7.0 %finish.1 = (bf16[12288,384]{1,0:T(8,128)(2,1)}, f32[384]{0:T(512)}, bf16[96,128]{1,0:T(8,128)(2,1)}) custom-call(f32[12288,384]{1,0:T(8,128)S(1)} %get-tuple-element.9.fresh, f32[1,384]{1,0:T(1,128)S(1)} %get-tuple-element.10.scale, f32[96,1,128]{2,1,0:T(1,128)S(1)} %get-tuple-element.11.norms), custom_call_target="tpu_custom_call" | custom-call | tf_op jit(solution)/shard_map/finish/pallas_call | solution.py:338

commit v3 on v2

--- a/solution.py
+++ b/solution.py
@@ -241,13 +241,10 @@
         c.wait_recv()
     get_rows.wait()
     add_block(chip, core)
-    take(0)
-    start(4)
-    take(1)
-    start(5)
-    take(2)
-    start(6)
-    for k in range(3, len(STAGES)):
+    for k in range(4, len(STAGES)):
+        take(k - 4)
+        start(k)
+    for k in range(len(STAGES) - 4, len(STAGES)):
         take(k)
     for k in range(len(STAGES) - AHEAD, len(STAGES)):
         for c in copies[k]:
@@ -264,12 +261,10 @@
     return (own_high[...].astype(jnp.float32) * mix_rate).astype(jnp.bfloat16)
 
 
-SLOTS = 4
+SLOTS = 8
 
 
 def finish(fresh, scale, norms, serve, scale_out, norm_out, slots, sems):
-    scale_out[...] = scale[...].reshape(COLS)
-    norm_out[...] = norms[...].reshape(D_MODEL // 128, 128).astype(jnp.bfloat16)
     inverse = jnp.broadcast_to(1.0 / scale[...], (8, COLS))
 
     def put(n, slot):
@@ -289,6 +284,8 @@
         return carry
 
     lax.fori_loop(0, GROUP, one, 0)
+    scale_out[...] = scale[...].reshape(COLS)
+    norm_out[...] = norms[...].reshape(D_MODEL // 128, 128).astype(jnp.bfloat16)
     for n in range(GROUP - SLOTS, GROUP):
         put(n, n % SLOTS).wait()
 

time: 126 us -> 123 us (0.976)
  Pallas kernels: 125 us -> 122 us
    pallas_call x1, Pallas kernels: 7 us -> 4.4 us  [per_device(): pl.pallas_call(finish, out_shape=(jax.ShapeDtypeStruct((D_MODEL, COLS), j...]
where the time goes in v3:
time: 123 us
  Pallas kernels  122 us (99%)
    pallas_call x1, Pallas kernels, per_device(): pl.pallas_call(exchange, out_shape=(pltpu.VMEM((D_MODEL, COLS), jnp.float...  118 us
    pallas_call x1, Pallas kernels, per_device(): pl.pallas_call(finish, out_shape=(jax.ShapeDtypeStruct((D_MODEL, COLS), j...  4.4 us

profile of v3, /device:TPU:0, one launch (start us, length us, event | category | flops | bytes accessed | tf_op | source)
XLA Modules:
  0.0 122.9 jit_solution(14462716157165869083)
XLA Ops:
  0.6 117.9 %exchange.1 = (f32[12288,384]{1,0:T(8,128)S(1)}, f32[1,384]{1,0:T(1,128)S(1)}, f32[96,1,128]{2,1,0:T(1,128)S(1)}) custom-call(bf16[384,12288]{1,0:T(8,128)(2,1)} %w.1, bf16[64,384]{1,0:T(8,128)(2,1)} %bitcast.4, bf16[64,12288]{1,0:T(8,128)(2,1)} %high.1, f32[1,96]{1,0:T(1,128)} %bitcast.5, f32[1,96]{1,0:T(1,128)} %bitcast.6), custom_call_target="tpu_custom_call" | custom-call | tf_op jit(solution)/shard_map/exchange/pallas_call | solution.py:300
  118.5 4.4 %finish.1 = (bf16[12288,384]{1,0:T(8,128)(2,1)}, f32[384]{0:T(512)}, bf16[96,128]{1,0:T(8,128)(2,1)}) custom-call(f32[12288,384]{1,0:T(8,128)S(1)} %get-tuple-element.9.fresh, f32[1,384]{1,0:T(1,128)S(1)} %get-tuple-element.10.scale, f32[96,1,128]{2,1,0:T(1,128)S(1)} %get-tuple-element.11.norms), custom_call_target="tpu_custom_call" | custom-call | tf_op jit(solution)/shard_map/finish/pallas_call | solution.py:335

commit v4 on v2

--- a/solution.py
+++ b/solution.py
@@ -61,6 +61,7 @@
     z = lax.axis_index("width")
     chip = y * SIDE + x
     me = chip * CORES + core
+    slow, fast = jnp.where(core == 0, y, x), jnp.where(core == 0, x, y)
 
     def at(dy, dx, dc):
         return lax.rem(y + dy, SIDE), lax.rem(x + dx, SIDE), lax.rem(core + dc, CORES)
@@ -70,27 +71,6 @@
 
     plane = [(dy, dx, dc) for dy in range(SIDE) for dx in range(SIDE) for dc in range(CORES)][1:]
     column = [(dz, dc) for dz in range(SIDE) for dc in range(CORES)][1:]
-
-    get_high = pltpu.make_async_copy(
-        high.at[:, pl.ds(pl.multiple_of(me * COLS, 128), COLS)], own_high, local.at[0]
-    )
-    get_high.start()
-    get_rows = pltpu.make_async_copy(
-        w.at[:, pl.ds(pl.multiple_of(me * COLS, 128), COLS)],
-        rows.at[pl.ds(pl.multiple_of(me * ROWS, ROWS), ROWS), :],
-        local.at[1],
-    )
-    get_rows.start()
-    get_low = pltpu.make_async_copy(
-        low.at[pl.ds(pl.multiple_of(z * PIECE, PIECE), PIECE), :], lows.at[z, core, chip], local.at[2]
-    )
-    get_low.start()
-    get_norms = [
-        pltpu.make_async_copy(part, norm_in.at[k], local.at[3 + k]) for k, part in enumerate((train, step))
-    ]
-    for c in get_norms:
-        c.start()
-    norm_own[...] = jnp.zeros_like(norm_own)
 
     barrier = pltpu.get_barrier_semaphore()
     for dy, dx, dc in plane:
@@ -98,25 +78,51 @@
     for dz, dc in column[1:]:
         to = device(y, x, lax.rem(core + dc, CORES), lax.rem(z + dz, SIDE))
         pl.semaphore_signal(barrier, inc=1, device_id=to, device_id_type=MESH)
+    get_high = pltpu.make_async_copy(
+        high.at[:, pl.ds(pl.multiple_of(me * COLS, 128), COLS)], own_high, local.at[0]
+    )
+    get_high.start()
+    get_rows = pltpu.make_async_copy(
+        w.at[:, pl.ds(pl.multiple_of(me * COLS, 128), COLS)],
+        rows.at[pl.ds(pl.multiple_of(me * ROWS, ROWS), ROWS), :],
+        local.at[1],
+    )
+    get_rows.start()
+    get_low = pltpu.make_async_copy(
+        low.at[pl.ds(pl.multiple_of(z * PIECE, PIECE), PIECE), :], lows.at[z, core, slow, fast], local.at[2]
+    )
+    get_low.start()
+    get_norms = [
+        pltpu.make_async_copy(part, norm_in.at[k], local.at[3 + k]) for k, part in enumerate((train, step))
+    ]
+    for c in get_norms:
+        c.start()
+    norm_own[...] = jnp.zeros_like(norm_own)
+
     pl.semaphore_wait(barrier, len(plane) + len(column) - 1)
 
-    low_copies = []
-    for k, (dy, dx, dc) in enumerate([h for h in plane if h[2] == 0]):
-        low_copies.append(
-            pltpu.make_async_remote_copy(
-                src_ref=low.at[pl.ds(pl.multiple_of(z * PIECE, PIECE), PIECE), :],
-                dst_ref=lows.at[z, core, chip],
-                send_sem=low_send.at[k],
-                recv_sem=low_recv.at[k],
-                device_id=device(*at(dy, dx, 0)),
-                device_id_type=MESH,
-            )
-        )
-    for c in low_copies:
-        c.start()
-    for c in get_norms:
-        c.wait()
-    norm_own[0, :, 0:NORM] = (norm_in[0] + norm_in[1]).astype(jnp.bfloat16).astype(jnp.float32)
+    def low_copy(k, t, source, target):
+        along, across = lax.rem(fast + t, SIDE), lax.rem(slow + t, SIDE)
+        if k == 0:
+            ty, tx = jnp.where(core == 0, y, along), jnp.where(core == 0, along, x)
+        else:
+            ty, tx = jnp.where(core == 0, across, y), jnp.where(core == 0, x, across)
+        return pltpu.make_async_remote_copy(
+            src_ref=source,
+            dst_ref=target,
+            send_sem=low_send.at[k * (SIDE - 1) + t - 1],
+            recv_sem=low_recv.at[k * (SIDE - 1) + t - 1],
+            device_id=device(ty, tx, core),
+            device_id_type=MESH,
+        )
+
+    own_low = low.at[pl.ds(pl.multiple_of(z * PIECE, PIECE), PIECE), :]
+    own_line = lows.at[z, core, slow]
+    low_first = [low_copy(0, t, own_low, lows.at[z, core, slow, fast]) for t in range(1, SIDE)]
+    low_then = [low_copy(1, t, own_line, own_line) for t in range(1, SIDE)]
+    low_copies = low_first + low_then
+    for c in low_first:
+        c.start()
     nz_copies = [
         pltpu.make_async_remote_copy(
             src_ref=norm_own.at[0],
@@ -152,8 +158,10 @@
 
     def add_block(source_chip, source_core):
         base = (source_chip * CORES + source_core) * ROWS
+        sy, sx = source_chip // SIDE, lax.rem(source_chip, SIDE)
+        line, place = jnp.where(source_core == 0, sy, sx), jnp.where(source_core == 0, sx, sy)
         for r in range(0, ROWS, STEP):
-            left = lows[:, source_core, source_chip, :, r : r + STEP].reshape(RANK, STEP)
+            left = lows[:, source_core, line, place, :, r : r + STEP].reshape(RANK, STEP)
             change = lax.dot_general(
                 left, own_high[...], (((0,), (0,)), ((), ())), preferred_element_type=jnp.float32
             )
@@ -187,12 +195,38 @@
     start(0)
     start(1)
 
+    for c in get_norms:
+        c.wait()
+    norm_own[0, :, 0:NORM] = (norm_in[0] + norm_in[1]).astype(jnp.bfloat16).astype(jnp.float32)
     for c in nz_copies:
         c.start()
     norm_z[z] = norm_own[0]
-    get_low.wait()
-    for c in low_copies:
-        c.wait_recv()
+    for c in nz_copies:
+        c.wait_recv()
+    lane = lax.broadcasted_iota(jnp.int32, (1, 128), 1)
+    second = pltpu.roll(norm_z[1], NORM, 1)
+    third = pltpu.roll(norm_z[2], 64, 1)
+    fourth = pltpu.roll(norm_z[3], 32, 1)
+    norm_mid[0] = jnp.where(lane < NORM, norm_z[0], second)
+    norm_mid[1] = jnp.where(lane < 64, second, third)
+    norm_mid[2] = jnp.where(lane < 32, third, fourth)
+    for j in range(3):
+        norms[me * 3 + j] = norm_mid[j]
+    own_high[...] = own_high_half(get_high, own_high)
+    total[...] = jnp.zeros_like(total)
+
+    start(2)
+    norm_copies = [
+        pltpu.make_async_remote_copy(
+            src_ref=norm_mid,
+            dst_ref=norms.at[pl.ds(me * 3, 3)],
+            send_sem=n_send.at[k],
+            recv_sem=n_recv.at[k],
+            device_id=device(*at(dy, dx, dc)),
+            device_id_type=MESH,
+        )
+        for k, (dy, dx, dc) in enumerate(plane)
+    ]
     low_zcopies = []
     for k, (dz, dc) in enumerate(column):
         low_zcopies.append(
@@ -205,50 +239,32 @@
                 device_id_type=MESH,
             )
         )
+    start(3)
+    get_low.wait()
+    for c in low_first:
+        c.wait_recv()
+    for c in low_then:
+        c.start()
+    start(4)
+    start(5)
+    for c in norm_copies:
+        c.start()
+    for c in low_then:
+        c.wait_recv()
     for c in low_zcopies:
         c.start()
-
-    for c in nz_copies:
-        c.wait_recv()
-    lane = lax.broadcasted_iota(jnp.int32, (1, 128), 1)
-    second = pltpu.roll(norm_z[1], NORM, 1)
-    third = pltpu.roll(norm_z[2], 64, 1)
-    fourth = pltpu.roll(norm_z[3], 32, 1)
-    norm_mid[0] = jnp.where(lane < NORM, norm_z[0], second)
-    norm_mid[1] = jnp.where(lane < 64, second, third)
-    norm_mid[2] = jnp.where(lane < 32, third, fourth)
-    for j in range(3):
-        norms[me * 3 + j] = norm_mid[j]
-    own_high[...] = own_high_half(get_high, own_high)
-    total[...] = jnp.zeros_like(total)
-
-    start(2)
-    norm_copies = [
-        pltpu.make_async_remote_copy(
-            src_ref=norm_mid,
-            dst_ref=norms.at[pl.ds(me * 3, 3)],
-            send_sem=n_send.at[k],
-            recv_sem=n_recv.at[k],
-            device_id=device(*at(dy, dx, dc)),
-            device_id_type=MESH,
-        )
-        for k, (dy, dx, dc) in enumerate(plane)
-    ]
-    for c in norm_copies:
-        c.start()
-    start(3)
+    start(6)
     for c in low_zcopies:
         c.wait_recv()
     get_rows.wait()
     add_block(chip, core)
     take(0)
-    start(4)
     take(1)
-    start(5)
     take(2)
-    start(6)
-    for k in range(3, len(STAGES)):
-        take(k)
+    take(3)
+    take(4)
+    take(5)
+    take(6)
     for k in range(len(STAGES) - AHEAD, len(STAGES)):
         for c in copies[k]:
             c.wait_send()
@@ -264,12 +280,10 @@
     return (own_high[...].astype(jnp.float32) * mix_rate).astype(jnp.bfloat16)
 
 
-SLOTS = 4
-
-
-def finish(fresh, scale, norms, serve, scale_out, norm_out, slots, sems):
-    scale_out[...] = scale[...].reshape(COLS)
-    norm_out[...] = norms[...].reshape(D_MODEL // 128, 128).astype(jnp.bfloat16)
+SLOTS = 8
+
+
+def finish(fresh, scale, norms, serve, scale_out, norm_out, slots, sems, scale_row, norm_rows, small):
     inverse = jnp.broadcast_to(1.0 / scale[...], (8, COLS))
 
     def put(n, slot):
@@ -288,7 +302,18 @@
         put(n, slot).start()
         return carry
 
-    lax.fori_loop(0, GROUP, one, 0)
+    lax.fori_loop(0, GROUP - SLOTS, one, 0)
+    scale_row[...] = scale[...].reshape(COLS)
+    norm_rows[...] = norms[...].reshape(D_MODEL // 128, 128).astype(jnp.bfloat16)
+    rest = [
+        pltpu.make_async_copy(scale_row, scale_out, small.at[0]),
+        pltpu.make_async_copy(norm_rows, norm_out, small.at[1]),
+    ]
+    for c in rest:
+        c.start()
+    lax.fori_loop(GROUP - SLOTS, GROUP, one, 0)
+    for c in rest:
+        c.wait()
     for n in range(GROUP - SLOTS, GROUP):
         put(n, n % SLOTS).wait()
 
@@ -296,7 +321,6 @@
 def per_device(w_up, low_up, high_up, norm_train, norm_step):
     dma = pltpu.SemaphoreType.DMA
     vmem = pl.BlockSpec(memory_space=pltpu.VMEM)
-    chips = CHIPS - 1
     column = SIDE * CORES - 1
     total = FIRST[-1]
     operands = (w_up, low_up.T, high_up, norm_train.reshape(1, NORM), norm_step.reshape(1, NORM))
@@ -311,7 +335,7 @@
         out_specs=(vmem,) * 3,
         scratch_shapes=[
             pltpu.VMEM((D_MODEL, COLS), jnp.bfloat16),
-            pltpu.VMEM((SIDE, CORES, CHIPS, PIECE, ROWS), jnp.bfloat16),
+            pltpu.VMEM((SIDE, CORES, SIDE, SIDE, PIECE, ROWS), jnp.bfloat16),
             pltpu.VMEM((RANK, COLS), jnp.bfloat16),
             pltpu.VMEM((2, 1, NORM), jnp.float32),
             pltpu.VMEM((1, 1, 128), jnp.float32),
@@ -320,8 +344,8 @@
             pltpu.VMEM((8, COLS), jnp.float32),
             dma((total,)),
             dma((total,)),
-            dma((chips,)),
-            dma((chips,)),
+            dma((2 * (SIDE - 1),)),
+            dma((2 * (SIDE - 1),)),
             dma((column,)),
             dma((column,)),
             dma((SIDE - 1,)),
@@ -343,8 +367,14 @@
             jax.ShapeDtypeStruct((D_MODEL // 128, 128), jnp.bfloat16),
         ),
         in_specs=[vmem] * 3,
-        out_specs=(pl.BlockSpec(memory_space=pltpu.HBM), vmem, vmem),
-        scratch_shapes=[pltpu.VMEM((SLOTS, ROWS, COLS), jnp.bfloat16), dma((SLOTS,))],
+        out_specs=(pl.BlockSpec(memory_space=pltpu.HBM),) * 3,
+        scratch_shapes=[
+            pltpu.VMEM((SLOTS, ROWS, COLS), jnp.bfloat16),
+            dma((SLOTS,)),
+            pltpu.VMEM((COLS,), jnp.float32),
+            pltpu.VMEM((D_MODEL // 128, 128), jnp.bfloat16),
+            dma((2,)),
+        ],
         compiler_params=pltpu.CompilerParams(vmem_limit_bytes=6 * 2**20),
         name="finish",
     )(*gathered)

time: 126 us -> 121 us (0.960)
  Pallas kernels: 125 us -> 120 us
    pallas_call x1, Pallas kernels: 7 us -> 3.8 us  [per_device(): pl.pallas_call(finish, out_shape=(jax.ShapeDtypeStruct((D_MODEL, COLS), j...]
    pallas_call x1, Pallas kernels: 118 us -> 116 us  [per_device(): pl.pallas_call(exchange, out_shape=(pltpu.VMEM((D_MODEL, COLS), jnp.float...]
where the time goes in v4:
time: 121 us
  Pallas kernels  120 us (99%)
    pallas_call x1, Pallas kernels, per_device(): pl.pallas_call(exchange, out_shape=(pltpu.VMEM((D_MODEL, COLS), jnp.float...  116 us
    pallas_call x1, Pallas kernels, per_device(): pl.pallas_call(finish, out_shape=(jax.ShapeDtypeStruct((D_MODEL, COLS), j...  3.8 us

profile of v4, /device:TPU:0, one launch (start us, length us, event | category | flops | bytes accessed | tf_op | source)
XLA Modules:
  0.0 120.9 jit_solution(13378820516960967068)
XLA Ops:
  0.6 116.5 %exchange.1 = (f32[12288,384]{1,0:T(8,128)S(1)}, f32[1,384]{1,0:T(1,128)S(1)}, f32[96,1,128]{2,1,0:T(1,128)S(1)}) custom-call(bf16[384,12288]{1,0:T(8,128)(2,1)} %w.1, bf16[64,384]{1,0:T(8,128)(2,1)} %bitcast.4, bf16[64,12288]{1,0:T(8,128)(2,1)} %high.1, f32[1,96]{1,0:T(1,128)} %bitcast.5, f32[1,96]{1,0:T(1,128)} %bitcast.6), custom_call_target="tpu_custom_call" | custom-call | tf_op jit(solution)/shard_map/exchange/pallas_call | solution.py:327
  117.1 3.8 %finish.1 = (bf16[12288,384]{1,0:T(8,128)(2,1)}, f32[384]{0:T(512)}, bf16[96,128]{1,0:T(8,128)(2,1)}) custom-call(f32[12288,384]{1,0:T(8,128)S(1)} %get-tuple-element.9.fresh, f32[1,384]{1,0:T(1,128)S(1)} %get-tuple-element.10.scale, f32[96,1,128]{2,1,0:T(1,128)S(1)} %get-tuple-element.11.norms), custom_call_target="tpu_custom_call" | custom-call | tf_op jit(solution)/shard_map/finish/pallas_call | solution.py:362

commit v5 on v4

--- a/solution.py
+++ b/solution.py
@@ -37,8 +37,8 @@
 STAGES = [
     hops((1, 1), (-1, -1)) + [((0, 0), (0, 0), 1)],
     hops((1, -1), (-1, 1)),
+    hops((2, 2)),
     hops((0, 2), (2, 0)),
-    hops((2, 2)),
     hops((1, 2), (-1, 2), (1, 0), (-1, 0)),
     hops(((2, 0), 1), ((2, 0), -1)),
     hops(((0, 2), 1), ((0, 2), -1)),
@@ -54,7 +54,7 @@
 def exchange(
     w, low, high, train, step,
     fresh_out, scale, norms,
-    rows, lows, own_high, norm_in, norm_own, norm_z, norm_mid, total,
+    rows, lows, own_high, norm_in, norm_own, norm_z, norm_mid, norm_all, total,
     send, recv, low_send, low_recv, low_zsend, low_zrecv, nz_send, nz_recv, n_send, n_recv, local,
 ):
     y, x, core = (lax.axis_index(a) for a in SHARD)
@@ -210,23 +210,30 @@
     norm_mid[0] = jnp.where(lane < NORM, norm_z[0], second)
     norm_mid[1] = jnp.where(lane < 64, second, third)
     norm_mid[2] = jnp.where(lane < 32, third, fourth)
-    for j in range(3):
-        norms[me * 3 + j] = norm_mid[j]
+    norm_all[core, y, x] = norm_mid[...]
     own_high[...] = own_high_half(get_high, own_high)
     total[...] = jnp.zeros_like(total)
 
     start(2)
-    norm_copies = [
-        pltpu.make_async_remote_copy(
-            src_ref=norm_mid,
-            dst_ref=norms.at[pl.ds(me * 3, 3)],
+    def norm_copy(k, source, target, to):
+        return pltpu.make_async_remote_copy(
+            src_ref=source,
+            dst_ref=target,
             send_sem=n_send.at[k],
             recv_sem=n_recv.at[k],
-            device_id=device(*at(dy, dx, dc)),
+            device_id=to,
             device_id_type=MESH,
         )
-        for k, (dy, dx, dc) in enumerate(plane)
+
+    norm_x = [
+        norm_copy(t - 1, norm_mid, norm_all.at[core, y, x], device(*at(0, t, 0))) for t in range(1, SIDE)
     ]
+    norm_y = [
+        norm_copy(t + 2, norm_all.at[core, y], norm_all.at[core, y], device(*at(t, 0, 0)))
+        for t in range(1, SIDE)
+    ]
+    norm_c = [norm_copy(6, norm_all.at[core], norm_all.at[core], device(*at(0, 0, 1)))]
+    norm_copies = norm_x + norm_y + norm_c
     low_zcopies = []
     for k, (dz, dc) in enumerate(column):
         low_zcopies.append(
@@ -243,15 +250,13 @@
     get_low.wait()
     for c in low_first:
         c.wait_recv()
-    for c in low_then:
+    for c in low_then + norm_x:
         c.start()
     start(4)
     start(5)
-    for c in norm_copies:
-        c.start()
-    for c in low_then:
-        c.wait_recv()
-    for c in low_zcopies:
+    for c in low_then + norm_x:
+        c.wait_recv()
+    for c in low_zcopies + norm_y:
         c.start()
     start(6)
     for c in low_zcopies:
@@ -263,15 +268,23 @@
     take(2)
     take(3)
     take(4)
+    for c in norm_y:
+        c.wait_recv()
+    for c in norm_c:
+        c.start()
     take(5)
+    for c in norm_c:
+        c.wait_recv()
+    for c in range(CORES):
+        for n in range(CHIPS):
+            k = (n * CORES + c) * 3
+            norms[k : k + 3] = norm_all[c, n // SIDE, n % SIDE]
     take(6)
     for k in range(len(STAGES) - AHEAD, len(STAGES)):
         for c in copies[k]:
             c.wait_send()
     for c in low_copies + low_zcopies + nz_copies + norm_copies:
         c.wait_send()
-    for c in norm_copies:
-        c.wait_recv()
     scale[...] = total[...].sum(axis=0, keepdims=True) / D_MODEL
 
 
@@ -341,6 +354,7 @@
             pltpu.VMEM((1, 1, 128), jnp.float32),
             pltpu.VMEM((SIDE, 1, 128), jnp.float32),
             pltpu.VMEM((3, 1, 128), jnp.float32),
+            pltpu.VMEM((CORES, SIDE, SIDE, 3, 1, 128), jnp.float32),
             pltpu.VMEM((8, COLS), jnp.float32),
             dma((total,)),
             dma((total,)),
@@ -350,8 +364,8 @@
             dma((column,)),
             dma((SIDE - 1,)),
             dma((SIDE - 1,)),
-            dma((GROUP - 1,)),
-            dma((GROUP - 1,)),
+            dma((2 * SIDE - 1,)),
+            dma((2 * SIDE - 1,)),
             dma((5,)),
         ],
         compiler_params=pltpu.CompilerParams(

time: 121 us -> 120 us (level)
    pallas_call x1, Pallas kernels: 116 us -> 115 us  [per_device(): pl.pallas_call(exchange, out_shape=(pltpu.VMEM((D_MODEL, COLS), jnp.float...]
where the time goes in v5:
time: 120 us
  Pallas kernels  119 us (99%)
    pallas_call x1, Pallas kernels, per_device(): pl.pallas_call(exchange, out_shape=(pltpu.VMEM((D_MODEL, COLS), jnp.float...  115 us
    pallas_call x1, Pallas kernels, per_device(): pl.pallas_call(finish, out_shape=(jax.ShapeDtypeStruct((D_MODEL, COLS), j...  3.8 us

profile of v5, /device:TPU:0, one launch (start us, length us, event | category | flops | bytes accessed | tf_op | source)
XLA Modules:
  0.0 119.6 jit_solution(7215102339163781825)
XLA Ops:
  0.6 115.2 %exchange.1 = (f32[12288,384]{1,0:T(8,128)S(1)}, f32[1,384]{1,0:T(1,128)S(1)}, f32[96,1,128]{2,1,0:T(1,128)S(1)}) custom-call(bf16[384,12288]{1,0:T(8,128)(2,1)} %w.1, bf16[64,384]{1,0:T(8,128)(2,1)} %bitcast.4, bf16[64,12288]{1,0:T(8,128)(2,1)} %high.1, f32[1,96]{1,0:T(1,128)} %bitcast.5, f32[1,96]{1,0:T(1,128)} %bitcast.6), custom_call_target="tpu_custom_call" | custom-call | tf_op jit(solution)/shard_map/exchange/pallas_call | solution.py:340
  115.8 3.8 %finish.1 = (bf16[12288,384]{1,0:T(8,128)(2,1)}, f32[384]{0:T(512)}, bf16[96,128]{1,0:T(8,128)(2,1)}) custom-call(f32[12288,384]{1,0:T(8,128)S(1)} %get-tuple-element.9.fresh, f32[1,384]{1,0:T(1,128)S(1)} %get-tuple-element.10.scale, f32[96,1,128]{2,1,0:T(1,128)S(1)} %get-tuple-element.11.norms), custom_call_target="tpu_custom_call" | custom-call | tf_op jit(solution)/shard_map/finish/pallas_call | solution.py:376

commit v6 on v5

--- a/solution.py
+++ b/solution.py
@@ -39,7 +39,7 @@
     hops((1, -1), (-1, 1)),
     hops((2, 2)),
     hops((0, 2), (2, 0)),
-    hops((1, 2), (-1, 2), (1, 0), (-1, 0)),
+    hops((1, 0), (-1, 0), (1, 2), (-1, 2)),
     hops(((2, 0), 1), ((2, 0), -1)),
     hops(((0, 2), 1), ((0, 2), -1)),
 ]

time: 120 us -> 120 us (level)
  no operation moved by 1% of the time
where the time goes in v6:
time: 120 us
  Pallas kernels  119 us (99%)
    pallas_call x1, Pallas kernels, per_device(): pl.pallas_call(exchange, out_shape=(pltpu.VMEM((D_MODEL, COLS), jnp.float...  115 us
    pallas_call x1, Pallas kernels, per_device(): pl.pallas_call(finish, out_shape=(jax.ShapeDtypeStruct((D_MODEL, COLS), j...  3.8 us

profile of v6, /device:TPU:0, one launch (start us, length us, event | category | flops | bytes accessed | tf_op | source)
XLA Modules:
  0.0 119.6 jit_solution(17342558240222686106)
XLA Ops:
  0.6 115.2 %exchange.1 = (f32[12288,384]{1,0:T(8,128)S(1)}, f32[1,384]{1,0:T(1,128)S(1)}, f32[96,1,128]{2,1,0:T(1,128)S(1)}) custom-call(bf16[384,12288]{1,0:T(8,128)(2,1)} %w.1, bf16[64,384]{1,0:T(8,128)(2,1)} %bitcast.4, bf16[64,12288]{1,0:T(8,128)(2,1)} %high.1, f32[1,96]{1,0:T(1,128)} %bitcast.5, f32[1,96]{1,0:T(1,128)} %bitcast.6), custom_call_target="tpu_custom_call" | custom-call | tf_op jit(solution)/shard_map/exchange/pallas_call | solution.py:340
  115.8 3.8 %finish.1 = (bf16[12288,384]{1,0:T(8,128)(2,1)}, f32[384]{0:T(512)}, bf16[96,128]{1,0:T(8,128)(2,1)}) custom-call(f32[12288,384]{1,0:T(8,128)S(1)} %get-tuple-element.9.fresh, f32[1,384]{1,0:T(1,128)S(1)} %get-tuple-element.10.scale, f32[96,1,128]{2,1,0:T(1,128)S(1)} %get-tuple-element.11.norms), custom_call_target="tpu_custom_call" | custom-call | tf_op jit(solution)/shard_map/finish/pallas_call | solution.py:376
